TPU v7x, 256 devices: a whole 4x4x8 slice. The times are simulated.
256 devices in a mesh: freq: 8 (over z_lo, x), panel: 32 (over z_hi, y, core).
Axes of the slice: x: 4, y: 4, z: 8 (z_hi: 4, z_lo: 2; z = z_hi * 2 + z_lo), core: 2. Of those that a mesh axis runs over, the one named last changes fastest.
Arguments:
- recorded: float32 [8, 2, 2048, 2048], P('freq', None, 'panel'), parts along dimension 0, may hold values from -60 to 60
- receiver_kernel: bfloat16 [8, 2, 4095], P('freq'), parts along dimension 0, may hold values from -1.5 to 1.5
- source_kernel: bfloat16 [8, 2, 4095], P('freq'), parts along dimension 0, may hold values from -1.5 to 1.5
Outputs:
- primaries: float32 [8, 2, 2048, 2048], P('freq', None, 'panel'), parts along dimension 0
- multiples: bfloat16 [8, 2, 2048, 2048], P('freq', None, 'panel'), parts along dimension 0
There are 8 independent parts, one for each index of `freq`. A program takes and returns all parts, laid end to end along the dimension named above; each array names one. Nothing has to cross between parts.
All inputs are finite; a program needn't handle non-finite values.
Results may differ from a plain program's by a relative error of at most 0.0057.
Values may be sent and summed in bfloat16 or wider, within the bound.
A program may use at most 320 MiB of HBM per device.

v0:
```python
import jax
import jax.numpy as jnp
from jax import lax
from jax.sharding import PartitionSpec as P


def from_everyone(value, axis):
    copies = jnp.broadcast_to(value, (lax.axis_size(axis), *value.shape))
    return lax.all_to_all(copies, axis, split_axis=0, concat_axis=0, tiled=True)


def over_copies(value, axis):
    everything = from_everyone(value, axis)
    return jnp.sum(everything, axis=0)


def packed_total(arrays, axis):
    flat, at, outs = (jnp.concatenate([a.reshape(-1) for a in arrays]), 0, [])
    running = over_copies(flat, axis)
    for a in arrays:
        outs.append(running[at : at + a.size].reshape(a.shape))
        at += a.size
    return tuple(outs)


def band(kernel, base, nrows, ncols):
    length = nrows + ncols - 1
    piece = lax.dynamic_slice_in_dim(kernel, base - nrows + 1, length, 1)
    rolled = jnp.roll(piece, -(nrows - 1), axis=1)
    flat = jnp.tile(rolled, (1, nrows))[:, : nrows * (length - 1)]
    return flat.reshape(2, nrows, length - 1)[:, :, :ncols]


def complex_dot(left, right):
    real_part = jnp.dot(left[0], right[0], preferred_element_type=jnp.float32) - jnp.dot(
        left[1], right[1], preferred_element_type=jnp.float32
    )
    imag_part = jnp.dot(left[0], right[1], preferred_element_type=jnp.float32) + jnp.dot(
        left[1], right[0], preferred_element_type=jnp.float32
    )
    return jnp.stack([real_part, imag_part])


def per_device(recorded, receiver_kernel, source_kernel):
    freqs, rows, width = (recorded.shape[0], recorded.shape[2], recorded.shape[3])
    panels = lax.axis_size("panel")
    sources = rows * panels
    data_b = recorded.astype(jnp.bfloat16)
    focused = jnp.stack(
        [complex_dot(data_b[0], band(receiver_kernel[0], width - 1, width, width))]
    ).astype(jnp.bfloat16)
    row_first = lax.axis_index("panel") * rows
    local_oper = jnp.stack([band(source_kernel[0], sources - 1 - row_first, rows, sources)])
    oper = local_oper[0]
    parts = [complex_dot(oper, lax.all_gather(focused, "panel", axis=2, tiled=True)[0])]
    summed = jnp.stack(parts)
    mult = summed.astype(jnp.bfloat16)
    mfl = mult.astype(jnp.float32)
    num_re = jnp.sum(mfl[:, 0] * recorded[:, 0] + mfl[:, 1] * recorded[:, 1], axis=(1, 2))
    num_im = jnp.sum(mfl[:, 0] * recorded[:, 1] - mfl[:, 1] * recorded[:, 0], axis=(1, 2))
    energy = jnp.sum(mfl[:, 0] * mfl[:, 0] + mfl[:, 1] * mfl[:, 1], axis=(1, 2))
    num_re, num_im, energy = packed_total((num_re, num_im, energy), "panel")
    den = energy + 1e-06
    fit_re = (num_re / den)[:, None, None]
    fit_im = (num_im / den)[:, None, None]
    prim_re = recorded[:, 0] - (fit_re * mfl[:, 0] - fit_im * mfl[:, 1])
    prim_im = recorded[:, 1] - (fit_re * mfl[:, 1] + fit_im * mfl[:, 0])
    return (jnp.stack([prim_re, prim_im], axis=1), mult)


def solution(mesh):
    placed = (P("freq", None, "panel", None), P("freq", None, None), P("freq", None, None))
    return jax.shard_map(
        per_device,
        mesh=mesh,
        in_specs=placed,
        out_specs=(P("freq", None, "panel", None), P("freq", None, "panel", None)),
        check_vma=False,
    )
```

profile of v0, /device:TPU:1, one launch (start us, length us, event | category | flops | bytes accessed | tf_op | source)
XLA Modules:
  0.0 450.9 jit_solution(5513023352090350222)
XLA Ops:
  7.2 0.0 copy-start
  7.2 0.0 all-gather.2.cloned.1.call-start
  7.2 0.8 slice.125
  8.0 0.7 slice.126
  8.7 11.1 %tile.20 = bf16[2,2048,4095]{2,1,0:T(8,128)(2,1)} broadcast(bf16[2,4095]{1,0:T(2,128)(2,1)S(1)} %pad_maximum_fusion.3), dimensions={0,2} | broadcast | bytes 33562620 | tf_op jit(solution)/shard_map/tile | solution.py:30
  19.8 69.4 %reshape.275 = bf16[16773120]{0:T(1024)(128)(2,1)} reshape(bf16[2,2048,4095]{2,1,0:T(8,128)(2,1)} %tile.20) | data formatting | bytes 67092480
  89.2 39.9 %tile.21 = bf16[2,8386560]{1,0:T(2,128)(2,1)} reshape(bf16[16773120]{0:T(1024)(128)(2,1)} %reshape.275) | data formatting | bytes 67092480 | tf_op jit(solution)/shard_map/tile | solution.py:30
  129.2 27.0 %slice.127 = bf16[2,8384512]{1,0:T(2,128)(2,1)} slice(bf16[2,8386560]{1,0:T(2,128)(2,1)} %tile.21), slice={[0:2], [0:8384512]} | slice | bytes 67076096 | tf_op jit(solution)/shard_map/slice | solution.py:30
  156.2 52.8 %reshape.277 = bf16[16769024]{0:T(1024)(128)(2,1)} reshape(bf16[2,8384512]{1,0:T(2,128)(2,1)} %slice.127) | data formatting | bytes 67076096
  209.0 0.0 copy-start.1
  209.0 53.1 %reshape.274 = bf16[2,2048,4094]{2,1,0:T(8,128)(2,1)} reshape(bf16[16769024]{0:T(1024)(128)(2,1)} %reshape.277) | data formatting | bytes 67076096 | tf_op jit(solution)/shard_map/reshape | solution.py:31
  262.1 0.0 copy-done.1
  262.1 0.1 convert_element_type.36
  262.2 4.9 %fusion = f32[2048,64]{0,1:T(8,128)S(1)} fusion(bf16[2,2048,4094]{2,1,0:T(8,128)(2,1)} %reshape.274, bf16[1,2,64,2048]{3,2,1,0:T(8,128)(2,1)S(1)} %convert_element_type.36), kind=kOutput, calls=%fused_computation.4 | convolution fusion | flops 536870912 | bytes 9175040 | tf_op jit(solution)/shard_map/dot_general | solution.py:35
  267.1 4.9 %fusion.1 = f32[2048,64]{0,1:T(8,128)S(1)} fusion(bf16[2,2048,4094]{2,1,0:T(8,128)(2,1)} %reshape.274, bf16[1,2,64,2048]{3,2,1,0:T(8,128)(2,1)S(1)} %convert_element_type.36), kind=kOutput, calls=%fused_computation.5 | convolution fusion | flops 536870912 | bytes 9175040 | tf_op jit(solution)/shard_map/dot_general | solution.py:38
  272.1 5.0 %fusion.19 = bf16[1,1,64,2048]{3,2,1,0:T(8,128)(2,1)S(1)} fusion(f32[2048,64]{0,1:T(8,128)S(1)} %fusion, bf16[2,2048,4094]{2,1,0:T(8,128)(2,1)} %reshape.274, bf16[1,2,64,2048]{3,2,1,0:T(8,128)(2,1)S(1)} %convert_element_type.36), kind=kOutput, calls=%fused_computation.23 | convolution fusion | flops 537133056 | bytes 9437184 | tf_op jit(solution)/shard_map/dot_general | solution.py:35
  277.0 5.0 %fusion.18 = bf16[1,1,64,2048]{3,2,1,0:T(8,128)(2,1)S(1)} fusion(f32[2048,64]{0,1:T(8,128)S(1)} %fusion.1, bf16[2,2048,4094]{2,1,0:T(8,128)(2,1)} %reshape.274, bf16[1,2,64,2048]{3,2,1,0:T(8,128)(2,1)S(1)} %convert_element_type.36), kind=kOutput, calls=%fused_computation.22 | convolution fusion | flops 537133056 | bytes 9437184 | tf_op jit(solution)/shard_map/dot_general | solution.py:38
  282.0 0.8 pad_maximum_fusion.1
  282.8 0.0 all-gather.2.cloned.1.call-update
  282.8 0.0 copy-done
  282.9 0.1 dynamic-slice_bitcast_fusion
  282.9 0.1 slice.120
  283.1 0.9 tile.9
  284.0 0.6 slice.122
  284.7 1.5 reshape.273
  286.2 106.4 %all-gather.2.cloned.1.call-done = bf16[1,2,2048,2048]{3,2,1,0:T(8,128)(2,1)} async-done(((bf16[1,2,64,2048]{3,2,1,0:T(8,128)(2,1)}), bf16[1,2,2048,2048]{3,2,1,0:T(8,128)(2,1)}) %all-gather.2.cloned.1.call-update) | async-done | bytes 16777232 | tf_op jit(solution)/shard_map/all_gather | solution.py:55
  392.6 0.0 copy-start.2
  392.6 5.1 %fusion.5 = f32[64,2048]{1,0:T(8,128)S(1)} fusion(bf16[1,2,2048,2048]{3,2,1,0:T(8,128)(2,1)} %all-gather.2.cloned.1.call-done, bf16[2,64,2110]{2,1,0:T(8,128)(2,1)S(1)} %reshape.273), kind=kOutput, calls=%fused_computation.9 | convolution fusion | flops 536870912 | bytes 9175040 | tf_op jit(solution)/shard_map/dot_general | solution.py:35
  397.7 5.7 %fusion.4 = f32[64,2048]{1,0:T(8,128)S(1)} fusion(bf16[1,2,2048,2048]{3,2,1,0:T(8,128)(2,1)} %all-gather.2.cloned.1.call-done, bf16[2,64,2110]{2,1,0:T(8,128)(2,1)S(1)} %reshape.273), kind=kOutput, calls=%fused_computation.8 | convolution fusion | flops 536870912 | bytes 9175040 | tf_op jit(solution)/shard_map/dot_general | solution.py:38
  403.4 0.0 copy-done.2
  403.4 1.6 fusion.16
  405.0 1.6 fusion.17
  406.6 0.9 fusion.20
  407.4 0.9 add_reduce_fusion.1
  408.4 2.0 pad_maximum_fusion.5
  410.4 29.6 %all_to_all.6 = f32[32,1,3]{2,1,0:T(1,128)S(1)} all-to-all(f32[32,1,3]{2,1,0:T(1,128)S(1)} %broadcast_in_dim.2), channel_id=1, replica_groups=mesh['freq'=8,'panel'=32] {'panel'}, dimensions={0} | all-to-all | bytes 768 | tf_op jit(solution)/shard_map/all_to_all | solution.py:9
  440.0 0.1 reduce_sum.48
  440.0 0.7 fusion.21
  442.6 0.2 subtract_subtract_fusion
  442.8 1.0 pad_maximum_fusion
  (5 shorter events, 0.1 us)
Async XLA Ops:
  7.2 275.7 %copy-start = (bf16[1,2,4095]{2,1,0:T(2,128)(2,1)S(1)}, bf16[1,2,4095]{2,1,0:T(2,128)(2,1)}, u32[]{:S(2)}) copy-start(bf16[1,2,4095]{2,1,0:T(2,128)(2,1)} %param.5) | copy-start | bytes 49144
  7.2 385.4 %all-gather.2.cloned.1.call-start = ((), (), s32[]{:S(2)}) async-start(), calls=%async_computation.1 | async-start | bytes 17301504 | tf_op jit(solution)/shard_map/all_gather | solution.py:55
  209.0 53.1 %copy-start.1 = (f32[1,2,64,2048]{3,2,1,0:T(8,128)S(1)}, f32[1,2,64,2048]{3,2,1,0:T(8,128)}, u32[]{:S(2)}) copy-start(f32[1,2,64,2048]{3,2,1,0:T(8,128)} %param.3) | copy-start | bytes 3145732
  392.6 10.8 %copy-start.2 = (bf16[1,2,2048,2048]{3,2,1,0:T(8,128)(2,1)S(1)}, bf16[1,2,2048,2048]{3,2,1,0:T(8,128)(2,1)}, u32[]{:S(2)}) copy-start(bf16[1,2,2048,2048]{3,2,1,0:T(8,128)(2,1)} %all-gather.2.cloned.1.call-done) | copy-start | bytes 50331652
Sparse Core Ops, SparseCore 0:
  283.0 109.5 all-gather.1
where the time goes:
time: 459 us; the launch traced here: 451 us
  local copies, waits for them, and re-layouts  259 us (56%)
  waiting for transfers between devices  106 us (23%)
  matrix products  33.7 us (7%)
  blocking collectives  29.6 us (6%)
  between operations  16.3 us (4%)
  other arithmetic  6.01 us (1%)
    unnamed x8, local copies, waits for them, and re-layouts  122 us
    all_gather x1, waiting for transfers between devices, per_device(): lax.all_gather(focused, 'panel', axis=2, tiled=True)[0]  106 us
    reshape x2, local copies, waits for them, and re-layouts, band(): return flat.reshape(2, nrows, length - 1)[:, :, :ncols]  54.6 us
    another operation x4, local copies, waits for them, and re-layouts, band(): flat = jnp.tile(rolled, (1, nrows))[:, :nrows * (length - 1)]  52 us
    all_to_all x1, blocking collectives, from_everyone(): return lax.all_to_all(copies, axis, split_axis=0, concat_axis=0, tiled=True)  29.6 us
    slice x2, local copies, waits for them, and re-layouts, band(): flat = jnp.tile(rolled, (1, nrows))[:, :nrows * (length - 1)]  27.7 us
    dot_general x2, matrix products, complex_dot(): jnp.dot(left[1], right[0], preferred_element_type=jnp.float32)  10.6 us
    dot_general x2, matrix products, complex_dot(): jnp.dot(left[0], right[0], preferred_element_type=jnp.float32)  10 us
  transfers between devices with their start and end apart: 1, of which 1 were waited for; matrix products, arithmetic and copies ran while one was open for 1% of the time, Pallas kernels for 0%

commit v1 on v0

--- a/solution.py
+++ b/solution.py
@@ -52,7 +52,14 @@
     row_first = lax.axis_index("panel") * rows
     local_oper = jnp.stack([band(source_kernel[0], sources - 1 - row_first, rows, sources)])
     oper = local_oper[0]
-    parts = [complex_dot(oper, lax.all_gather(focused, "panel", axis=2, tiled=True)[0])]
+
+    def finish_plane(field_in, a_name, ndim_at):
+        inter = jax.lax.axis_size(a_name)
+        carry = jnp.stack([field_in] * inter)
+        z = jax.lax.all_to_all(carry, a_name, 0, 0)
+        return jnp.concatenate(z, ndim_at)
+
+    parts = [complex_dot(oper, finish_plane(focused, "panel", 2)[0])]
     summed = jnp.stack(parts)
     mult = summed.astype(jnp.bfloat16)
     mfl = mult.astype(jnp.float32)

time: 459 us -> 705 us (1.54)
  waiting for transfers between devices: 106 us -> 363 us
  blocking collectives: 29.6 us -> 14.9 us
  between operations: 16.3 us -> 2.97 us
  local copies, waits for them, and re-layouts: 259 us -> 272 us
  starting transfers between devices: 0.04 us -> 13 us
  matrix products: 33.7 us -> 26.3 us
    all_to_all x0 -> x1, waiting for transfers between devices: none -> 363 us  [finish_plane(): z = jax.lax.all_to_all(carry, a_name, 0, 0)]
    all_gather x1 -> x0, waiting for transfers between devices: 106 us -> none  [per_device(): lax.all_gather(focused, 'panel', axis=2, tiled=True)[0]]
    all_to_all x1, blocking collectives: 29.6 us -> 14.9 us  [from_everyone(): return lax.all_to_all(copies, axis, split_axis=0, concat_axis=0, tiled=True)]
    all_to_all x0 -> x1, starting transfers between devices: none -> 13 us  [finish_plane(): z = jax.lax.all_to_all(carry, a_name, 0, 0)]
    unnamed x8 -> x6, local copies, waits for them, and re-layouts: 122 us -> 122 us
  transfers between devices with their start and end apart: 1 -> 1, of which waited for: 1 -> 1; matrix products, arithmetic and copies ran while one was open for 1% -> 0% of each run, Pallas kernels for 0% -> 0%
where the time goes in v1:
time: 705 us; the launch traced here: 696 us
  waiting for transfers between devices  363 us (51%)
  local copies, waits for them, and re-layouts  272 us (39%)
  matrix products  26.3 us (4%)
  blocking collectives  14.9 us (2%)
  starting transfers between devices  13 us (2%)
    all_to_all x1, waiting for transfers between devices, finish_plane(): z = jax.lax.all_to_all(carry, a_name, 0, 0)  363 us
    unnamed x6, local copies, waits for them, and re-layouts  122 us
    reshape x2, local copies, waits for them, and re-layouts, band(): return flat.reshape(2, nrows, length - 1)[:, :, :ncols]  54.6 us
    another operation x4, local copies, waits for them, and re-layouts, band(): flat = jnp.tile(rolled, (1, nrows))[:, :nrows * (length - 1)]  52 us
    slice x2, local copies, waits for them, and re-layouts, band(): flat = jnp.tile(rolled, (1, nrows))[:, :nrows * (length - 1)]  27.4 us
    all_to_all x1, blocking collectives, from_everyone(): return lax.all_to_all(copies, axis, split_axis=0, concat_axis=0, tiled=True)  14.9 us
  transfers between devices with their start and end apart: 1, of which 1 were waited for; matrix products, arithmetic and copies ran while one was open for 0% of the time, Pallas kernels for 0%

profile of v1, /device:TPU:1, one launch (start us, length us, event | category | flops | bytes accessed | tf_op | source)
XLA Modules:
  0.0 696.4 jit_solution(6827613463282353877)
XLA Ops:
  0.6 0.0 copy-start
  0.6 0.8 slice.125
  1.4 0.7 slice.126
  2.2 11.1 %tile.20 = bf16[2,2048,4095]{2,1,0:T(8,128)(2,1)} broadcast(bf16[2,4095]{1,0:T(2,128)(2,1)S(1)} %pad_maximum_fusion.3), dimensions={0,2} | broadcast | bytes 33562620 | tf_op jit(solution)/shard_map/tile | solution.py:30
  13.2 69.4 %reshape.275 = bf16[16773120]{0:T(1024)(128)(2,1)} reshape(bf16[2,2048,4095]{2,1,0:T(8,128)(2,1)} %tile.20) | data formatting | bytes 67092480
  82.6 39.9 %tile.21 = bf16[2,8386560]{1,0:T(2,128)(2,1)} reshape(bf16[16773120]{0:T(1024)(128)(2,1)} %reshape.275) | data formatting | bytes 67092480 | tf_op jit(solution)/shard_map/tile | solution.py:30
  122.6 27.0 %slice.127 = bf16[2,8384512]{1,0:T(2,128)(2,1)} slice(bf16[2,8386560]{1,0:T(2,128)(2,1)} %tile.21), slice={[0:2], [0:8384512]} | slice | bytes 67076096 | tf_op jit(solution)/shard_map/slice | solution.py:30
  149.6 52.8 %reshape.277 = bf16[16769024]{0:T(1024)(128)(2,1)} reshape(bf16[2,8384512]{1,0:T(2,128)(2,1)} %slice.127) | data formatting | bytes 67076096
  202.4 0.0 copy-start.1
  202.4 53.1 %reshape.273 = bf16[2,2048,4094]{2,1,0:T(8,128)(2,1)} reshape(bf16[16769024]{0:T(1024)(128)(2,1)} %reshape.277) | data formatting | bytes 67076096 | tf_op jit(solution)/shard_map/reshape | solution.py:31
  255.5 0.0 copy-done.1
  255.5 0.1 convert_element_type.35
  255.6 4.9 fusion
  260.5 4.9 fusion.1
  265.5 5.0 fusion.13
  270.4 5.0 fusion.12
  275.4 0.1 pad_maximum_fusion.1
  275.5 6.0 stack.19
  281.5 13.0 %all-to-all-start = ((bf16[32,1,2,64,2048]{4,3,2,1,0:T(8,128)(2,1)}), bf16[32,1,2,64,2048]{4,3,2,1,0:T(8,128)(2,1)}, u32[]{:S(2)}, u32[]{:S(2)}) async-start(bf16[32,1,2,64,2048]{4,3,2,1,0:T(8,128)(2,1)} %stack.19), calls=%async_computation | async-start | bytes 33554432 | tf_op jit(solution)/shard_map/all_to_all | solution.py:59
  294.5 0.0 copy-done
  294.5 0.1 dynamic-slice_bitcast_fusion
  294.6 0.1 slice.120
  294.7 0.9 tile.9
  295.7 0.4 slice.122
  296.1 1.5 reshape.272
  297.6 362.5 %all-to-all-done = bf16[32,1,2,64,2048]{4,3,2,1,0:T(8,128)(2,1)} async-done(((bf16[32,1,2,64,2048]{4,3,2,1,0:T(8,128)(2,1)}), bf16[32,1,2,64,2048]{4,3,2,1,0:T(8,128)(2,1)}, u32[]{:S(2)}, u32[]{:S(2)}) %all-to-all-start) | async-done | bytes 16777248 | tf_op jit(solution)/shard_map/all_to_all | solution.py:59
  660.2 7.0 fusion.17
  667.1 1.6 fusion.15
  668.7 1.6 fusion.14
  670.4 1.6 fusion.11
  672.0 1.6 fusion.10
  673.6 0.9 fusion.16
  674.5 0.9 add_reduce_fusion.1
  675.5 2.0 pad_maximum_fusion.5
  677.5 14.9 %all_to_all.11 = f32[32,1,3]{2,1,0:T(1,128)S(1)} all-to-all(f32[32,1,3]{2,1,0:T(1,128)S(1)} %broadcast_in_dim.2), channel_id=1, replica_groups=mesh['freq'=8,'panel'=32] {'panel'}, dimensions={0} | all-to-all | bytes 768 | tf_op jit(solution)/shard_map/all_to_all | solution.py:9
  692.3 0.1 reduce_sum.48
  692.4 0.7 fusion.18
  695.0 0.2 subtract_subtract_fusion
  695.1 1.0 pad_maximum_fusion
  (5 shorter events, 0.1 us)
Async XLA Ops:
  0.6 293.8 %copy-start = (bf16[1,2,4095]{2,1,0:T(2,128)(2,1)S(1)}, bf16[1,2,4095]{2,1,0:T(2,128)(2,1)}, u32[]{:S(2)}) copy-start(bf16[1,2,4095]{2,1,0:T(2,128)(2,1)} %param.5) | copy-start | bytes 49144
  202.4 53.1 %copy-start.1 = (f32[1,2,64,2048]{3,2,1,0:T(8,128)S(1)}, f32[1,2,64,2048]{3,2,1,0:T(8,128)}, u32[]{:S(2)}) copy-start(f32[1,2,64,2048]{3,2,1,0:T(8,128)} %param.3) | copy-start | bytes 3145732
  281.5 378.7 %all-to-all-start = ((bf16[32,1,2,64,2048]{4,3,2,1,0:T(8,128)(2,1)}), bf16[32,1,2,64,2048]{4,3,2,1,0:T(8,128)(2,1)}, u32[]{:S(2)}, u32[]{:S(2)}) async-start(bf16[32,1,2,64,2048]{4,3,2,1,0:T(8,128)(2,1)} %stack.19), calls=%async_computation | async-start | bytes 33554432 | tf_op jit(solution)/shard_map/all_to_all | solution.py:59
